TPU v7x, 256 devices: a whole 4x4x8 slice. The times are simulated.
256 devices in a mesh: row: 16 (over z, core), col: 16 (over y, x).
Axes of the slice: x: 4, y: 4, z: 8, core: 2. Of those that a mesh axis runs over, the one named last changes fastest.
Arguments:
- act_codes: int32 [2048, 7168], P('col', 'row'), may hold values from -127 to 127
- act_scales: float32 [2048, 112], P('col', 'row'), may hold values from 0.005 to 0.03
- gate_weight: bfloat16 [7168, 18432], P('row', 'col'), may hold values from -0.0625 to 0.0625
- up_weight: bfloat16 [7168, 18432], P('row', 'col'), may hold values from -0.0625 to 0.0625
- down_weight: bfloat16 [18432, 7168], P('col', 'row'), may hold values from -0.046875 to 0.046875
Outputs:
- mixed: bfloat16 [2048, 7168], P('col', 'row')
All inputs are finite; a program needn't handle non-finite values.
Results may differ from a plain program's by a relative error of at most 0.03.
Values may be sent and summed in bfloat16 or wider, within the bound.
A program may use at most 128 MiB of HBM per device.

v0:
```python
import jax
import jax.numpy as jnp
from jax import lax
from jax.sharding import Mesh
from jax.sharding import PartitionSpec as P

ROW = ("row_0", "row_1")


def in_order(tiles, dim):
    tiles = jnp.moveaxis(tiles, 0, dim)
    lengths = tiles.shape
    return tiles.reshape(*lengths[:dim], lengths[dim] * lengths[dim + 1], *lengths[dim + 2 :])


def sent_to_all(array, axis):
    copies = jnp.broadcast_to(array, (lax.axis_size(axis), *array.shape))
    return lax.all_to_all(copies, axis, split_axis=0, concat_axis=0, tiled=True)


def gather_directly(array, axis, dim):
    return in_order(sent_to_all(array, axis), dim)


def own_block(tiles, axes, order):
    lengths = [lax.axis_size(a) for a in axes]
    tiles = tiles.reshape(*lengths, *tiles.shape[1:])
    tiles = tiles.transpose(*order, *range(len(axes), tiles.ndim))
    tiles = tiles.reshape(-1, *tiles.shape[len(axes) :])
    for k in order:
        tiles = lax.psum_scatter(tiles, axes[k], scatter_dimension=0, tiled=True)
    return tiles[0]


def cut_along(array, dim, length):
    before, after = (array.shape[:dim], array.shape[dim + 1 :])
    return jnp.moveaxis(array.reshape(*before, length, -1, *after), dim, 0)


def scatter_axes(array, axes, order, dim):
    length = lax.axis_size(axes)
    return own_block(cut_along(array, dim, length), axes, order)


def sent_and_summed(array, axis, dim):
    length = lax.axis_size(axis)
    tiles = lax.all_to_all(cut_along(array, dim, length), axis, 0, 0, tiled=True)
    return jnp.sum(tiles.astype(jnp.float32), axis=0)


def on_device(act_codes, act_scales, gate_weight, up_weight, down_weight):
    local_rows = act_codes.shape[0]
    width = act_codes.shape[1]
    nblocks = act_scales.shape[1]
    blocked = act_codes.astype(jnp.float32).reshape(local_rows, nblocks, width // nblocks)
    acts = (blocked * act_scales[:, :, None]).reshape(local_rows, width).astype(jnp.bfloat16)
    every = gather_directly(acts, "col", 0)
    hidden_width = gate_weight.shape[1]
    gate_part = jnp.dot(every, gate_weight, preferred_element_type=jnp.float32)
    up_part = jnp.dot(every, up_weight, preferred_element_type=jnp.float32)
    summed = scatter_axes(
        jnp.concatenate([gate_part, up_part], axis=1).astype(jnp.bfloat16), ROW, (1, 0), 0
    ).astype(jnp.float32)
    hidden = (jax.nn.silu(summed[:, :hidden_width]) * summed[:, hidden_width:]).astype(jnp.bfloat16)
    partial_value = jnp.dot(
        lax.all_gather(hidden, ROW, axis=0, tiled=True),
        down_weight,
        preferred_element_type=jnp.float32,
    )
    mixed = sent_and_summed(partial_value.astype(jnp.bfloat16), "col", 0)
    return mixed.astype(jnp.bfloat16)


def solution(mesh):
    torus = Mesh(mesh.devices.reshape(8, 2, mesh.shape["col"]), ("row_0", "row_1", "col"))
    in_specs = (P("col", ROW), P("col", ROW), P(ROW, "col"), P(ROW, "col"), P("col", ROW))
    out_specs = P("col", ROW)
    return jax.shard_map(
        on_device, mesh=torus, in_specs=in_specs, out_specs=out_specs, check_vma=False
    )
```

profile of v0, /device:TPU:1, one launch (start us, length us, event | category | flops | bytes accessed | tf_op | source)
XLA Modules:
  0.0 233.5 jit_solution(17031267609659101783)
XLA Ops:
  6.5 0.0 copy-start
  6.5 0.0 reduce-scatter.3.cloned.1.call-start
  6.5 1.1 fusion.4
  7.6 0.3 broadcast_in_dim.4
  8.0 32.1 %all_to_all.10 = bf16[16,128,448]{1,2,0:T(8,128)(2,1)S(1)} all-to-all(bf16[16,128,448]{1,2,0:T(8,128)(2,1)S(1)} %broadcast_in_dim.4), channel_id=1, replica_groups=mesh['row_0'=8,'row_1'=2,'col'=16] {'col'}, dimensions={0} | all-to-all | bytes 3670016 | tf_op jit(solution)/shard_map/all_to_all | solution.py:18
  40.1 0.0 copy-start.1
  40.1 0.0 copy-done
  40.1 3.2 %convolution_convert_fusion = bf16[8,2,128,1152]{3,2,1,0:T(8,128)(2,1)S(1)} fusion(bf16[8,2,128,448]{2,3,1,0:T(8,128)(2,1)S(1)} %bitcast.32, bf16[448,1152]{1,0:T(8,128)(2,1)S(1)} %copy-done), kind=kOutput, calls=%fused_computation.1 | convolution fusion | flops 2116288512 | bytes 7585792 | tf_op jit(solution)/shard_map/dot_general | solution.py:60
  43.3 0.0 copy-done.1
  43.3 3.2 %convolution_convert_fusion.1 = bf16[8,2,128,1152]{3,2,1,0:T(8,128)(2,1)S(1)} fusion(bf16[8,2,128,448]{2,3,1,0:T(8,128)(2,1)S(1)} %bitcast.33, bf16[448,1152]{1,0:T(8,128)(2,1)S(1)} %copy-done.1), kind=kOutput, calls=%fused_computation.2 | convolution fusion | flops 2116288512 | bytes 7585792 | tf_op jit(solution)/shard_map/dot_general | solution.py:59
  46.4 4.0 %maximum_bitcast_fusion = bf16[2,8,128,2304]{3,2,0,1:T(8,128)(2,1)} fusion(bf16[8,2,128,1152]{3,2,1,0:T(8,128)(2,1)S(1)} %convolution_convert_fusion, bf16[8,2,128,1152]{3,2,1,0:T(8,128)(2,1)S(1)} %convolution_convert_fusion.1), kind=kLoop, calls=%fused_computation | loop fusion | flops 18874368 | bytes 18874368 | tf_op jit(solution)/shard_map/transpose | solution.py:28
  50.5 8.1 %copy.7 = bf16[2,8,128,2304]{3,2,1,0:T(8,128)(2,1)} copy(bf16[2,8,128,2304]{3,2,0,1:T(8,128)(2,1)} %maximum_bitcast_fusion) | data formatting | bytes 18874368 | tf_op jit(solution)/shard_map/transpose | solution.py:28
  58.6 0.0 reduce-scatter.3.cloned.1.call-update
  58.6 0.0 copy-start.2
  58.6 0.0 reduce-scatter.5.cloned.1.call-start
  58.7 23.4 %reduce-scatter.3.cloned.1.call-done = bf16[8,128,2304]{2,1,0:T(8,128)(2,1)} async-done(((bf16[16,128,2304]{2,1,0:T(8,128)(2,1)}), bf16[8,128,2304]{2,1,0:T(8,128)(2,1)}) %reduce-scatter.3.cloned.1.call-update) | async-done | bytes 4718608 | tf_op jit(solution)/shard_map/reduce_scatter | solution.py:31
  82.1 0.0 reduce-scatter.5.cloned.1.call-update
  82.1 0.0 all-gather.2.cloned.1.call-start
  82.1 63.5 %reduce-scatter.5.cloned.1.call-done = bf16[1,128,2304]{2,1,0:T(8,128)(2,1)} async-done(((bf16[8,128,2304]{2,1,0:T(8,128)(2,1)}), bf16[1,128,2304]{2,1,0:T(8,128)(2,1)}) %reduce-scatter.5.cloned.1.call-update) | async-done | bytes 589840 | tf_op jit(solution)/shard_map/reduce_scatter | solution.py:31
  145.7 1.1 bitcast_convert_fusion
  146.8 0.9 fusion.3
  147.7 0.0 all-gather.2.cloned.1.call-update
  147.7 41.5 %all-gather.2.cloned.1.call-done = bf16[2048,1152]{1,0:T(8,128)(2,1)} async-done(((bf16[128,1152]{1,0:T(8,128)(2,1)}), bf16[2048,1152]{1,0:T(8,128)(2,1)}) %all-gather.2.cloned.1.call-update) | async-done | bytes 4718608 | tf_op jit(solution)/shard_map/all_gather | solution.py:66
  189.2 0.0 copy-done.2
  189.2 4.9 %fusion = bf16[56,16,8,128]{3,2,1,0:T(8,128)(2,1)S(1)} fusion(bf16[2048,1152]{1,0:T(8,128)(2,1)} %all-gather.2.cloned.1.call-done, bf16[1152,448]{0,1:T(8,128)(2,1)S(1)} %copy-done.2), kind=kOutput, calls=%fused_computation.5 | convolution fusion | flops 2114846720 | bytes 7585792 | tf_op jit(solution)/shard_map/dot_general | solution.py:65
  194.1 0.5 copy.13
  194.6 31.5 %all_to_all.11 = bf16[16,128,448]{1,2,0:T(8,128)(2,1)S(1)} all-to-all(bf16[16,128,448]{1,2,0:T(8,128)(2,1)S(1)} %bitcast.31), channel_id=1, replica_groups=mesh['row_0'=8,'row_1'=2,'col'=16] {'col'}, dimensions={0} | all-to-all | bytes 3670016 | tf_op jit(solution)/shard_map/all_to_all | solution.py:47
  226.1 0.9 reduce_sum.12
Async XLA Ops:
  6.5 33.6 %copy-start = (bf16[448,1152]{1,0:T(8,128)(2,1)S(1)}, bf16[448,1152]{1,0:T(8,128)(2,1)}, u32[]{:S(2)}) copy-start(bf16[448,1152]{1,0:T(8,128)(2,1)} %param.8) | copy-start | bytes 3096580
  6.5 75.5 %reduce-scatter.3.cloned.1.call-start = ((), (), s32[]{:S(2)}) async-start(), calls=%async_computation.4 | async-start | bytes 14155776 | tf_op jit(solution)/shard_map/reduce_scatter | solution.py:31
  40.1 3.2 %copy-start.1 = (bf16[448,1152]{1,0:T(8,128)(2,1)S(1)}, bf16[448,1152]{1,0:T(8,128)(2,1)}, u32[]{:S(2)}) copy-start(bf16[448,1152]{1,0:T(8,128)(2,1)} %param.7) | copy-start | bytes 3096580
  58.6 130.6 %copy-start.2 = (bf16[1152,448]{0,1:T(8,128)(2,1)S(1)}, bf16[1152,448]{0,1:T(8,128)(2,1)}, u32[]{:S(2)}) copy-start(bf16[1152,448]{0,1:T(8,128)(2,1)} %param.9) | copy-start | bytes 3096580
  58.6 87.0 %reduce-scatter.5.cloned.1.call-start = ((), (), s32[]{:S(2)}) async-start(), calls=%async_computation.5 | async-start | bytes 5308416 | tf_op jit(solution)/shard_map/reduce_scatter | solution.py:31
  82.1 107.1 %all-gather.2.cloned.1.call-start = ((), (), s32[]{:S(2)}) async-start(), calls=%async_computation.6 | async-start | bytes 5013504 | tf_op jit(solution)/shard_map/all_gather | solution.py:66
Sparse Core Ops, SparseCore 0:
  58.7 23.2 reduce-scatter.2
  84.6 60.9 reduce-scatter.4
  147.9 41.2 all-gather.1
where the time goes:
time: 234 us; the launch traced here: 233 us
  waiting for transfers between devices  128 us (55%)
  blocking collectives  63.6 us (27%)
  between operations  13.2 us (6%)
  matrix products  11.2 us (5%)
  local copies, waits for them, and re-layouts  8.97 us (4%)
  other arithmetic  8.02 us (3%)
    reduce_scatter x2, waiting for transfers between devices, own_block(): tiles = lax.psum_scatter(tiles, axes[k], scatter_dimension=0, tiled=True)  86.9 us
    all_gather x1, waiting for transfers between devices, on_device(): lax.all_gather(hidden, ROW, axis=0, tiled=True)  41.5 us
    all_to_all x1, blocking collectives, sent_to_all(): return lax.all_to_all(copies, axis, split_axis=0, concat_axis=0, tiled=True)  32.1 us
    all_to_all x1, blocking collectives, sent_and_summed(): lax.all_to_all(cut_along(array, dim, length), axis, 0, 0, tiled=True)  31.5 us
    transpose x1, local copies, waits for them, and re-layouts, own_block(): tiles = tiles.transpose(*order, *range(len(axes), tiles.ndim))  8.14 us
    dot_general x1, matrix products, on_device(): jnp.dot(lax.all_gather(hidden, ROW, axis=0, tiled=True), down_weight, pre...  4.9 us
  transfers between devices with their start and end apart: 3, of which 3 were waited for; matrix products, arithmetic and copies ran while one was open for 0% of the time, Pallas kernels for 0%

commit v1 on v0

--- a/solution.py
+++ b/solution.py
@@ -5,6 +5,13 @@
 from jax.sharding import PartitionSpec as P
 
 ROW = ("row_0", "row_1")
+
+
+def swapped_in(shard, mesh_axis, along):
+    size = lax.axis_size(mesh_axis)
+    shards = jnp.stack([shard for _ in range(size)])
+    shards = lax.all_to_all(shards, mesh_axis, split_axis=0, concat_axis=0)
+    return jnp.concatenate(shards, axis=along)
 
 
 def in_order(tiles, dim):
@@ -63,9 +70,7 @@
     ).astype(jnp.float32)
     hidden = (jax.nn.silu(summed[:, :hidden_width]) * summed[:, hidden_width:]).astype(jnp.bfloat16)
     partial_value = jnp.dot(
-        lax.all_gather(hidden, ROW, axis=0, tiled=True),
-        down_weight,
-        preferred_element_type=jnp.float32,
+        swapped_in(hidden, ROW, 0), down_weight, preferred_element_type=jnp.float32
     )
     mixed = sent_and_summed(partial_value.astype(jnp.bfloat16), "col", 0)
     return mixed.astype(jnp.bfloat16)

time: 234 us -> 303 us (1.29)
  blocking collectives: 63.6 us -> 176 us
  waiting for transfers between devices: 128 us -> 87 us
    all_to_all x0 -> x1, blocking collectives: none -> 112 us  [swapped_in(): shards = lax.all_to_all(shards, mesh_axis, split_axis=0, concat_axis=0)]
    all_gather x1 -> x0, waiting for transfers between devices: 41.5 us -> none  [on_device(): lax.all_gather(hidden, ROW, axis=0, tiled=True)]
  transfers between devices with their start and end apart: 3 -> 2, of which waited for: 3 -> 2; matrix products, arithmetic and copies ran while one was open for 0% -> 0% of each run, Pallas kernels for 0% -> 0%
where the time goes in v1:
time: 303 us; the launch traced here: 302 us
  blocking collectives  176 us (58%)
  waiting for transfers between devices  87 us (29%)
  between operations  13.5 us (4%)
  local copies, waits for them, and re-layouts  9.59 us (3%)
  matrix products  8.9 us (3%)
  other arithmetic  7.31 us (2%)
    all_to_all x1, blocking collectives, swapped_in(): shards = lax.all_to_all(shards, mesh_axis, split_axis=0, concat_axis=0)  112 us
    reduce_scatter x2, waiting for transfers between devices, own_block(): tiles = lax.psum_scatter(tiles, axes[k], scatter_dimension=0, tiled=True)  87 us
    all_to_all x1, blocking collectives, sent_to_all(): return lax.all_to_all(copies, axis, split_axis=0, concat_axis=0, tiled=True)  32.1 us
    all_to_all x1, blocking collectives, sent_and_summed(): lax.all_to_all(cut_along(array, dim, length), axis, 0, 0, tiled=True)  31.8 us
    transpose x1, local copies, waits for them, and re-layouts, own_block(): tiles = tiles.transpose(*order, *range(len(axes), tiles.ndim))  8.13 us
  transfers between devices with their start and end apart: 2, of which 2 were waited for; matrix products, arithmetic and copies ran while one was open for 0% of the time, Pallas kernels for 0%

profile of v1, /device:TPU:1, one launch (start us, length us, event | category | flops | bytes accessed | tf_op | source)
XLA Modules:
  0.0 302.4 jit_solution(16204802959289999047)
XLA Ops:
  6.5 0.0 copy-start
  6.5 0.0 reduce-scatter.3.cloned.1.call-start
  6.5 1.1 fusion.4
  7.6 0.3 broadcast_in_dim.4
  8.0 32.1 %all_to_all.15 = bf16[16,128,448]{1,2,0:T(8,128)(2,1)S(1)} all-to-all(bf16[16,128,448]{1,2,0:T(8,128)(2,1)S(1)} %broadcast_in_dim.4), channel_id=1, replica_groups=mesh['row_0'=8,'row_1'=2,'col'=16] {'col'}, dimensions={0} | all-to-all | bytes 3670016 | tf_op jit(solution)/shard_map/all_to_all | solution.py:25
  40.1 0.0 copy-start.1
  40.1 0.0 copy-done
  40.1 3.2 %convolution_convert_fusion = bf16[8,2,128,1152]{3,2,1,0:T(8,128)(2,1)S(1)} fusion(bf16[8,2,128,448]{2,3,1,0:T(8,128)(2,1)S(1)} %bitcast.34, bf16[448,1152]{1,0:T(8,128)(2,1)S(1)} %copy-done), kind=kOutput, calls=%fused_computation.1 | convolution fusion | flops 2116288512 | bytes 7585792 | tf_op jit(solution)/shard_map/dot_general | solution.py:67
  43.3 0.0 copy-done.1
  43.3 3.2 %convolution_convert_fusion.1 = bf16[8,2,128,1152]{3,2,1,0:T(8,128)(2,1)S(1)} fusion(bf16[8,2,128,448]{2,3,1,0:T(8,128)(2,1)S(1)} %bitcast.35, bf16[448,1152]{1,0:T(8,128)(2,1)S(1)} %copy-done.1), kind=kOutput, calls=%fused_computation.2 | convolution fusion | flops 2116288512 | bytes 7585792 | tf_op jit(solution)/shard_map/dot_general | solution.py:66
  46.4 4.0 %maximum_bitcast_fusion = bf16[2,8,128,2304]{3,2,0,1:T(8,128)(2,1)} fusion(bf16[8,2,128,1152]{3,2,1,0:T(8,128)(2,1)S(1)} %convolution_convert_fusion, bf16[8,2,128,1152]{3,2,1,0:T(8,128)(2,1)S(1)} %convolution_convert_fusion.1), kind=kLoop, calls=%fused_computation | loop fusion | flops 18874368 | bytes 18874368 | tf_op jit(solution)/shard_map/transpose | solution.py:35
  50.5 8.1 %copy.7 = bf16[2,8,128,2304]{3,2,1,0:T(8,128)(2,1)} copy(bf16[2,8,128,2304]{3,2,0,1:T(8,128)(2,1)} %maximum_bitcast_fusion) | data formatting | bytes 18874368 | tf_op jit(solution)/shard_map/transpose | solution.py:35
  58.6 0.0 reduce-scatter.3.cloned.1.call-update
  58.6 0.0 reduce-scatter.5.cloned.1.call-start
  58.7 23.4 %reduce-scatter.3.cloned.1.call-done = bf16[8,128,2304]{2,1,0:T(8,128)(2,1)} async-done(((bf16[16,128,2304]{2,1,0:T(8,128)(2,1)}), bf16[8,128,2304]{2,1,0:T(8,128)(2,1)}) %reduce-scatter.3.cloned.1.call-update) | async-done | bytes 4718608 | tf_op jit(solution)/shard_map/reduce_scatter | solution.py:38
  82.1 0.0 reduce-scatter.5.cloned.1.call-update
  82.1 63.6 %reduce-scatter.5.cloned.1.call-done = bf16[1,128,2304]{2,1,0:T(8,128)(2,1)} async-done(((bf16[8,128,2304]{2,1,0:T(8,128)(2,1)}), bf16[1,128,2304]{2,1,0:T(8,128)(2,1)}) %reduce-scatter.5.cloned.1.call-update) | async-done | bytes 589840 | tf_op jit(solution)/shard_map/reduce_scatter | solution.py:38
  145.7 1.1 bitcast_convert_fusion
  146.8 0.2 fusion.3
  147.0 0.6 stack.2
  147.6 0.0 copy-start.2
  147.6 112.1 %all_to_all.16 = bf16[16,128,1152]{2,1,0:T(8,128)(2,1)S(1)} all-to-all(bf16[16,128,1152]{2,1,0:T(8,128)(2,1)S(1)} %stack.2), channel_id=1, replica_groups=mesh['row_0'=8,'row_1'=2,'col'=16] {'row_0','row_1'}, dimensions={0} | all-to-all | bytes 9437184 | tf_op jit(solution)/shard_map/all_to_all | solution.py:13
  259.8 0.0 copy-done.2
  259.8 2.6 fusion
  262.3 0.5 copy.13
  262.8 31.8 %all_to_all.17 = bf16[16,128,448]{1,2,0:T(8,128)(2,1)S(1)} all-to-all(bf16[16,128,448]{1,2,0:T(8,128)(2,1)S(1)} %bitcast.32), channel_id=1, replica_groups=mesh['row_0'=8,'row_1'=2,'col'=16] {'col'}, dimensions={0} | all-to-all | bytes 3670016 | tf_op jit(solution)/shard_map/all_to_all | solution.py:54
  294.6 0.9 reduce_sum.12
Async XLA Ops:
  6.5 33.6 %copy-start = (bf16[448,1152]{1,0:T(8,128)(2,1)S(1)}, bf16[448,1152]{1,0:T(8,128)(2,1)}, u32[]{:S(2)}) copy-start(bf16[448,1152]{1,0:T(8,128)(2,1)} %param.8) | copy-start | bytes 3096580
  6.5 75.5 %reduce-scatter.3.cloned.1.call-start = ((), (), s32[]{:S(2)}) async-start(), calls=%async_computation.5 | async-start | bytes 14155776 | tf_op jit(solution)/shard_map/reduce_scatter | solution.py:38
  40.1 3.2 %copy-start.1 = (bf16[448,1152]{1,0:T(8,128)(2,1)S(1)}, bf16[448,1152]{1,0:T(8,128)(2,1)}, u32[]{:S(2)}) copy-start(bf16[448,1152]{1,0:T(8,128)(2,1)} %param.7) | copy-start | bytes 3096580
  58.6 87.0 %reduce-scatter.5.cloned.1.call-start = ((), (), s32[]{:S(2)}) async-start(), calls=%async_computation.6 | async-start | bytes 5308416 | tf_op jit(solution)/shard_map/reduce_scatter | solution.py:38
  147.6 112.1 %copy-start.2 = (bf16[1152,448]{0,1:T(8,128)(2,1)S(1)}, bf16[1152,448]{0,1:T(8,128)(2,1)}, u32[]{:S(2)}) copy-start(bf16[1152,448]{0,1:T(8,128)(2,1)} %param.9) | copy-start | bytes 3096580
Sparse Core Ops, SparseCore 0:
  58.7 23.2 reduce-scatter.2
  84.6 60.9 reduce-scatter.4
